TPU v7x, 128 devices: a whole 4x4x4 slice. The times are simulated.
128 devices in a mesh: fsdp: 32 (over x, y, core), dp: 4 (over z).
Axes of the slice: x: 4, y: 4, z: 4, core: 2. Of those that a mesh axis runs over, the one named last changes fastest.
Arguments:
- tokens: bfloat16 [65536, 4096], P(('fsdp', 'dp')), may hold values from -40 to 40
- cotangent: bfloat16 [65536, 2048], P(('fsdp', 'dp')), may hold values from -20 to 20
- weight: bfloat16 [4096, 2048], P('fsdp'), may hold values from -1 to 1
- left_vector: float32 [4096], P('fsdp'), may hold values from -6 to 6
Outputs:
- layer_out: bfloat16 [65536, 2048], P(('fsdp', 'dp'))
- input_grad: bfloat16 [65536, 4096], P(('fsdp', 'dp'))
- update: bfloat16 [4096, 2048], P('fsdp')
- left_next: float32 [4096], P('fsdp')
- right_next: float32 [2048], replicated
All inputs are finite; a program needn't handle non-finite values.
Results may differ from a plain program's by a relative error of at most 0.015.
Values may be sent and summed in bfloat16 or wider, within the bound.
A program may use at most 128 MiB of HBM per device.

v0:
```python
import jax
import jax.numpy as jnp
from jax import lax
from jax.sharding import Mesh
from jax.sharding import PartitionSpec as P

FSDP = ("fsdp_0", "fsdp_1", "fsdp_2")
FSDP_DP = ("fsdp_0", "fsdp_1", "fsdp_2", "dp")
epsilon = 1e-06


def sent_to_all(value, axis):
    copies = jnp.broadcast_to(value, (lax.axis_size(axis), *value.shape))
    return lax.all_to_all(copies, axis, split_axis=0, concat_axis=0, tiled=True)


def taken_together(value, axis):
    return sent_to_all(value, axis).sum(axis=0)


def in_order(blocks, dim):
    blocks = jnp.moveaxis(blocks, 0, dim)
    dims = blocks.shape
    return blocks.reshape(*dims[:dim], dims[dim] * dims[dim + 1], *dims[dim + 2 :])


def gather_in_order(value, axes, order):
    blocks = value[None]
    for k in order:
        blocks = lax.all_gather(blocks, axes[k], axis=0, tiled=True)
    block = [lax.axis_size(axes[k]) for k in reversed(order)]
    blocks = blocks.reshape(*block, *value.shape)
    turned = sorted(range(len(order)), key=lambda place: order[len(order) - 1 - place])
    return blocks.transpose(*turned, *range(len(order), blocks.ndim)).reshape(-1, *value.shape)


def whole_of(value, axes, order, dim):
    return in_order(gather_in_order(value, axes, order), dim)


def over_copies(value, axis):
    everything = sent_to_all(value, axis)
    return jnp.sum(everything.astype(jnp.float32), axis=0)


def packed_total(arrays, axis):
    flat, at, done = (jnp.concatenate([a.reshape(-1) for a in arrays]), 0, [])
    running = taken_together(flat, axis)
    for a in arrays:
        done.append(running[at : at + a.size].reshape(a.shape))
        at += a.size
    return tuple(done)


def per_device(tokens, cotangent, weight, left_vector):
    weight_wide = weight.astype(jnp.float32)
    part_right = jnp.dot(left_vector, weight_wide)
    right_raw = taken_together(part_right, FSDP)
    right_next = right_raw / jnp.sqrt(jnp.sum(right_raw * right_raw) + epsilon)
    left_raw = jnp.dot(weight_wide, right_next)
    left_sq = taken_together(jnp.sum(left_raw * left_raw), FSDP)
    spectral = jnp.sqrt(left_sq + epsilon)
    left_next = left_raw / spectral
    gathered = whole_of(weight, (("fsdp_0", "fsdp_1"), "fsdp_2"), (0, 1), 0)
    product = jnp.dot(tokens, gathered, preferred_element_type=jnp.float32)
    layer_out = (product / spectral).astype(jnp.bfloat16)
    back_prod = lax.dot_general(
        cotangent, gathered, (((1,), (1,)), ((), ())), preferred_element_type=jnp.float32
    )
    input_grad = (back_prod / spectral).astype(jnp.bfloat16)
    shard_rows = weight.shape[0]
    shard_sum = lax.psum_scatter(
        lax.dot_general(
            tokens, cotangent, (((0,), (0,)), ((), ())), preferred_element_type=jnp.float32
        ).astype(jnp.bfloat16),
        FSDP,
        scatter_dimension=0,
        tiled=True,
    )
    grad_sum = over_copies(shard_sum, "dp").astype(jnp.float32)
    entry_count = shard_rows * lax.axis_size(FSDP) * weight.shape[1]
    along_right = jnp.dot(grad_sum, right_next)
    grad_sq_raw, inner_prod, cross_term = packed_total(
        (
            jnp.sum(grad_sum * grad_sum),
            jnp.sum(grad_sum * weight_wide),
            jnp.sum(left_next * along_right),
        ),
        FSDP,
    )
    rank_coeff = inner_prod / (spectral * spectral)
    gradient = grad_sum / spectral - rank_coeff * left_next[:, None] * right_next[None, :]
    left_unit = left_sq / (left_sq + epsilon)
    right_unit = jnp.sum(right_next * right_next)
    grad_sq = (
        grad_sq_raw / (spectral * spectral)
        - 2.0 * rank_coeff * cross_term / spectral
        + rank_coeff * rank_coeff * left_unit * right_unit
    )
    grad_rms = jnp.sqrt(grad_sq / entry_count + epsilon)
    update = (gradient / grad_rms).astype(jnp.bfloat16)
    return (layer_out, input_grad, update, left_next, right_next)


def solution(mesh):
    torus = Mesh(
        mesh.devices.reshape(4, 4, 2, mesh.shape["dp"]), ("fsdp_0", "fsdp_1", "fsdp_2", "dp")
    )
    placed = (P(FSDP_DP, None), P(FSDP_DP, None), P(FSDP, None), P(FSDP))
    return jax.shard_map(
        per_device,
        mesh=torus,
        in_specs=placed,
        out_specs=(P(FSDP_DP, None), P(FSDP_DP, None), P(FSDP, None), P(FSDP), P()),
        check_vma=False,
    )
```

profile of v0, /device:TPU:1, one launch (start us, length us, event | category | flops | bytes accessed | tf_op | source)
XLA Modules:
  0.0 247.7 jit_solution(5602320976544870512)
XLA Ops:
  8.0 0.0 copy-start
  8.0 0.0 all-gather.6.cloned.1.call-start
  8.1 0.7 all-gather.6.cloned.1.call-update
  8.7 0.0 reduce-scatter.2.cloned.1.call-start
  8.8 0.8 copy-done
  9.6 14.6 %convolution_convert_fusion = bf16[4096,2048]{1,0:T(8,128)(2,1)} fusion(bf16[512,4096]{1,0:T(8,128)(2,1)} %param.4, bf16[512,2048]{1,0:T(8,128)(2,1)S(1)} %copy-done), kind=kOutput, calls=%fused_computation | convolution fusion | flops 8598323200 | bytes 23068672 | tf_op jit(solution)/shard_map/dot_general | solution.py:73
  24.2 0.0 reduce-scatter.2.cloned.1.call-update
  24.2 0.0 all-gather.4.cloned.1.call-start
  24.3 60.4 %all-gather.6.cloned.1.call-done = bf16[2048,2048]{1,0:T(8,128)(2,1)} async-done(((bf16[128,2048]{1,0:T(8,128)(2,1)}), bf16[2048,2048]{1,0:T(8,128)(2,1)}) %all-gather.6.cloned.1.call-update) | async-done | bytes 8388624 | tf_op jit(solution)/shard_map/all_gather | solution.py:30
  84.7 0.0 copy-start.2
  84.7 0.0 copy-start.5
  84.7 0.0 all-gather.4.cloned.1.call-update
  84.7 1.0 copy-done.2
  85.7 0.0 copy-done.5
  85.7 0.2 fusion.6
  85.9 0.1 broadcast_in_dim.18
  86.1 17.9 %all_to_all.23 = f32[32,1,2048]{2,1,0:T(1,128)S(1)} all-to-all(f32[32,1,2048]{2,1,0:T(1,128)S(1)} %broadcast_in_dim.18), channel_id=1, replica_groups=mesh['fsdp_0'=4,'fsdp_1'=4,'fsdp_2'=2,'dp'=4] {'fsdp_0','fsdp_1','fsdp_2'}, dimensions={0} | all-to-all | bytes 524288 | tf_op jit(solution)/shard_map/all_to_all | solution.py:14
  103.9 0.2 reduce_sum.90
  104.1 0.6 multiply_reduce_fusion.3
  105.4 0.6 multiply_reduce_fusion.2
  106.0 0.0 copy-start.3
  106.0 0.8 multiply_reduce_fusion.4
  106.9 0.7 broadcast_in_dim.19
  107.5 10.9 %all_to_all.24 = f32[32,1,1]{2,1,0:T(1,128)S(1)} all-to-all(f32[32,1,1]{2,1,0:T(1,128)S(1)} %broadcast_in_dim.19), channel_id=1, replica_groups=mesh['fsdp_0'=4,'fsdp_1'=4,'fsdp_2'=2,'dp'=4] {'fsdp_0','fsdp_1','fsdp_2'}, dimensions={0} | all-to-all | bytes 256 | tf_op jit(solution)/shard_map/all_to_all | solution.py:14
  118.4 26.0 %reduce-scatter.2.cloned.1.call-done = bf16[128,2048]{1,0:T(8,128)(2,1)} async-done(((bf16[4096,2048]{1,0:T(8,128)(2,1)}), bf16[128,2048]{1,0:T(8,128)(2,1)}) %reduce-scatter.2.cloned.1.call-update) | async-done | bytes 524304 | tf_op jit(solution)/shard_map/reduce_scatter | solution.py:72
  144.4 2.6 %broadcast_in_dim.20 = bf16[4,128,2048]{2,1,0:T(8,128)(2,1)} broadcast(bf16[128,2048]{1,0:T(8,128)(2,1)} %reduce-scatter.2.cloned.1.call-done), dimensions={1,2} | broadcast | bytes 2621440 | tf_op jit(solution)/shard_map/broadcast_in_dim | solution.py:13
  147.0 4.4 %all-to-all-start.2 = ((bf16[4,128,2048]{2,1,0:T(8,128)(2,1)}), bf16[4,128,2048]{2,1,0:T(8,128)(2,1)}, u32[]{:S(2)}, u32[]{:S(2)}) async-start(bf16[4,128,2048]{2,1,0:T(8,128)(2,1)} %broadcast_in_dim.20), calls=%async_computation.3 | async-start | bytes 4194304 | tf_op jit(solution)/shard_map/all_to_all | solution.py:14
  151.5 0.7 reduce_sum.93
  152.8 0.0 copy-start.4
  152.8 23.0 %all-to-all-done.2 = bf16[4,128,2048]{2,1,0:T(8,128)(2,1)} async-done(((bf16[4,128,2048]{2,1,0:T(8,128)(2,1)}), bf16[4,128,2048]{2,1,0:T(8,128)(2,1)}, u32[]{:S(2)}, u32[]{:S(2)}) %all-to-all-start.2) | async-done | bytes 2097184 | tf_op jit(solution)/shard_map/all_to_all | solution.py:14
  175.8 2.1 convert_reduce_fusion
  177.9 0.9 fusion.1
  178.8 1.9 multiply_reduce_fusion.1
  180.7 1.9 pad_maximum_fusion
  182.6 0.6 broadcast_in_dim.21
  183.2 8.0 %all-to-all-start.3 = ((f32[32,1,3]{2,1,0:T(1,128)}), f32[32,1,3]{2,1,0:T(1,128)S(1)}, u32[]{:S(2)}, u32[]{:S(2)}) async-start(f32[32,1,3]{2,1,0:T(1,128)} %broadcast_in_dim.21), calls=%async_computation.4 | async-start | bytes 32768 | tf_op jit(solution)/shard_map/all_to_all | solution.py:14
  191.9 6.3 %all-to-all-done.3 = f32[32,1,3]{2,1,0:T(1,128)S(1)} async-done(((f32[32,1,3]{2,1,0:T(1,128)}), f32[32,1,3]{2,1,0:T(1,128)S(1)}, u32[]{:S(2)}, u32[]{:S(2)}) %all-to-all-start.3) | async-done | bytes 416 | tf_op jit(solution)/shard_map/all_to_all | solution.py:14
  198.1 0.1 reduce_sum.98
  198.2 0.6 fusion.5
  201.4 0.0 copy-done.3
  201.4 1.0 divide_convert_fusion.2
  202.4 0.0 all-gather.4.cloned.1.call-done
  202.4 0.0 copy-start.6
  202.4 8.3 %copy.16 = bf16[16,2,128,2048]{3,2,1,0:T(8,128)(2,1)S(1)} copy(bf16[16,2,128,2048]{3,2,0,1:T(8,128)(2,1)} %bitcast.45) | data formatting | bytes 33554432 | tf_op jit(solution)/shard_map/transpose | solution.py:34
  210.7 0.0 copy-done.4
  210.7 0.0 copy-start.1
  210.7 5.7 %copy-done.1 = bf16[16,2,128,2048]{3,2,1,0:T(8,128)(2,1)} copy-done((bf16[16,2,128,2048]{3,2,1,0:T(8,128)(2,1)}, bf16[16,2,128,2048]{3,2,1,0:T(8,128)(2,1)S(1)}, u32[]{:S(2)}) %copy-start.1) | copy-done | bytes 16777240
  216.4 0.0 copy-done.6
  216.4 10.1 %divide_convert_fusion.1 = bf16[512,2048]{1,0:T(8,128)(2,1)} fusion(bf16[512,4096]{1,0:T(8,128)(2,1)S(1)} %copy-done.6, bf16[4096,2048]{1,0:T(8,128)(2,1)S(1)} %bitcast.46, f32[]{:T(128)S(6)} %sqrt.10), kind=kOutput, calls=%fused_computation.3 | convolution fusion | flops 8592031744 | bytes 23068676 | tf_op jit(solution)/shard_map/dot_general | solution.py:65
  226.5 13.8 %divide_convert_fusion = bf16[512,4096]{1,0:T(8,128)(2,1)} fusion(bf16[512,2048]{1,0:T(8,128)(2,1)S(1)} %copy-done, bf16[4096,2048]{1,0:T(8,128)(2,1)} %bitcast.47, f32[]{:T(128)S(6)} %sqrt.10), kind=kOutput, calls=%fused_computation.1 | convolution fusion | flops 8594128896 | bytes 23068676 | tf_op jit(solution)/shard_map/dot_general | solution.py:67
  (2 shorter events, 0.0 us)
Async XLA Ops:
  8.0 1.6 copy-start
  8.0 76.7 %all-gather.6.cloned.1.call-start = ((), (), s32[]{:S(2)}) async-start(), calls=%async_computation.7 | async-start | bytes 8912896 | tf_op jit(solution)/shard_map/all_gather | solution.py:30
  8.7 135.7 %reduce-scatter.2.cloned.1.call-start = ((), (), s32[]{:S(2)}) async-start(), calls=%async_computation.6 | async-start | bytes 17301504 | tf_op jit(solution)/shard_map/reduce_scatter | solution.py:72
  24.2 178.2 %all-gather.4.cloned.1.call-start = ((), (), s32[]{:S(2)}) async-start(), calls=%async_computation.5 | async-start | bytes 25165824 | tf_op jit(solution)/shard_map/all_gather | solution.py:30
  84.7 1.0 copy-start.2
  84.7 1.0 copy-start.5
  106.0 95.4 %copy-start.3 = (f32[2048]{0:T(1024)}, f32[2048]{0:T(1024)S(1)}, u32[]{:S(2)}) copy-start(f32[2048]{0:T(1024)S(1)} %get-tuple-element.8) | copy-start | bytes 24580
  147.0 28.8 %all-to-all-start.2 = ((bf16[4,128,2048]{2,1,0:T(8,128)(2,1)}), bf16[4,128,2048]{2,1,0:T(8,128)(2,1)}, u32[]{:S(2)}, u32[]{:S(2)}) async-start(bf16[4,128,2048]{2,1,0:T(8,128)(2,1)} %broadcast_in_dim.20), calls=%async_computation.3 | async-start | bytes 4194304 | tf_op jit(solution)/shard_map/all_to_all | solution.py:14
  152.8 57.9 %copy-start.4 = (f32[128]{0:T(128)}, f32[128]{0:T(128)S(1)}, u32[]{:S(2)}) copy-start(f32[128]{0:T(128)S(1)} %broadcast_divide_fusion.1) | copy-start | bytes 1540
  183.2 14.9 %all-to-all-start.3 = ((f32[32,1,3]{2,1,0:T(1,128)}), f32[32,1,3]{2,1,0:T(1,128)S(1)}, u32[]{:S(2)}, u32[]{:S(2)}) async-start(f32[32,1,3]{2,1,0:T(1,128)} %broadcast_in_dim.21), calls=%async_computation.4 | async-start | bytes 32768 | tf_op jit(solution)/shard_map/all_to_all | solution.py:14
  202.4 14.0 %copy-start.6 = (bf16[512,4096]{1,0:T(8,128)(2,1)S(1)}, bf16[512,4096]{1,0:T(8,128)(2,1)}, u32[]{:S(2)}) copy-start(bf16[512,4096]{1,0:T(8,128)(2,1)} %param.4) | copy-start | bytes 12582916
  210.7 5.7 %copy-start.1 = (bf16[16,2,128,2048]{3,2,1,0:T(8,128)(2,1)}, bf16[16,2,128,2048]{3,2,1,0:T(8,128)(2,1)S(1)}, u32[]{:S(2)}) copy-start(bf16[16,2,128,2048]{3,2,1,0:T(8,128)(2,1)S(1)} %copy.16) | copy-start | bytes 50331652
Sparse Core Ops, SparseCore 0:
  11.0 73.6 all-gather.5
  86.3 33.1 all-gather.3
Sparse Core Ops, SparseCore 1:
  24.3 120.0 reduce-scatter.1
where the time goes:
time: 248 us
  waiting for transfers between devices  116 us (47%)
  matrix products  40.3 us (16%)
  blocking collectives  28.8 us (12%)
  local copies, waits for them, and re-layouts  20.4 us (8%)
  between operations  20.2 us (8%)
  starting transfers between devices  12.6 us (5%)
  other arithmetic  9.01 us (4%)
    all_gather x2, waiting for transfers between devices, gather_in_order(): blocks = lax.all_gather(blocks, axes[k], axis=0, tiled=True)  60.4 us
    all_to_all x2, waiting for transfers between devices, sent_to_all(): return lax.all_to_all(copies, axis, split_axis=0, concat_axis=0, tiled=True)  29.3 us
    all_to_all x2, blocking collectives, sent_to_all(): return lax.all_to_all(copies, axis, split_axis=0, concat_axis=0, tiled=True)  28.8 us
    reduce_scatter x1, waiting for transfers between devices, per_device(): lax.psum_scatter(lax.dot_general(tokens, cotangent, (((0,), (0,)), ((), (...  26 us
    dot_general x1, matrix products, per_device(): lax.dot_general(tokens, cotangent, (((0,), (0,)), ((), ())), preferred_el...  14.6 us
    dot_general x1, matrix products, per_device(): lax.dot_general(cotangent, gathered, (((1,), (1,)), ((), ())), preferred_...  13.8 us
    all_to_all x2, starting transfers between devices, sent_to_all(): return lax.all_to_all(copies, axis, split_axis=0, concat_axis=0, tiled=True)  12.5 us
    dot_general x1, matrix products, per_device(): product = jnp.dot(tokens, gathered, preferred_element_type=jnp.float32)  10.1 us
  transfers between devices with their start and end apart: 5, of which 4 were waited for; matrix products, arithmetic and copies ran while one was open for 12% of the time, Pallas kernels for 0%

commit v1 on v0

--- a/solution.py
+++ b/solution.py
@@ -27,7 +27,9 @@
 def gather_in_order(value, axes, order):
     blocks = value[None]
     for k in order:
-        blocks = lax.all_gather(blocks, axes[k], axis=0, tiled=True)
+        blocks = jnp.concatenate(
+            lax.all_to_all(jnp.stack([blocks] * lax.axis_size(axes[k])), axes[k], 0, 0), axis=0
+        )
     block = [lax.axis_size(axes[k]) for k in reversed(order)]
     blocks = blocks.reshape(*block, *value.shape)
     turned = sorted(range(len(order)), key=lambda place: order[len(order) - 1 - place])

time: 248 us -> 349 us (1.41)
  waiting for transfers between devices: 116 us -> 163 us
  blocking collectives: 28.8 us -> 47.2 us
  starting transfers between devices: 12.6 us -> 26 us
  other arithmetic: 9.01 us -> 18.8 us
  local copies, waits for them, and re-layouts: 20.4 us -> 28.8 us
  matrix products: 40.3 us -> 45 us
    all_to_all x0 -> x1, waiting for transfers between devices: none -> 148 us  [gather_in_order(): lax.all_to_all(jnp.stack([blocks] * lax.axis_size(axes[k])), axes[k], 0, 0)]
    all_gather x2 -> x0, waiting for transfers between devices: 60.4 us -> none  [gather_in_order(): blocks = lax.all_gather(blocks, axes[k], axis=0, tiled=True)]
    reduce_scatter x1, waiting for transfers between devices: 26 us -> 5.87 us  [per_device(): lax.psum_scatter(lax.dot_general(tokens, cotangent, (((0,), (0,)), ((), (...]
    all_to_all x2, waiting for transfers between devices: 29.3 us -> 9.71 us  [sent_to_all(): return lax.all_to_all(copies, axis, split_axis=0, concat_axis=0, tiled=True)]
    all_to_all x0 -> x1, blocking collectives: none -> 19.5 us  [gather_in_order(): lax.all_to_all(jnp.stack([blocks] * lax.axis_size(axes[k])), axes[k], 0, 0)]
    another operation x0 -> x1, other arithmetic: none -> 9.73 us  [gather_in_order(): jnp.stack([blocks] * lax.axis_size(axes[k]))]
    all_to_all x2, starting transfers between devices: 12.5 us -> 21.2 us  [sent_to_all(): return lax.all_to_all(copies, axis, split_axis=0, concat_axis=0, tiled=True)]
    transpose x1 -> x0, local copies, waits for them, and re-layouts: 8.26 us -> none  [gather_in_order(): blocks.transpose(*turned, *range(len(order), blocks.ndim))]
  transfers between devices with their start and end apart: 5 -> 4, of which waited for: 4 -> 3; matrix products, arithmetic and copies ran while one was open for 12% -> 18% of each run, Pallas kernels for 0% -> 0%
where the time goes in v1:
time: 349 us; the launch traced here: 348 us
  waiting for transfers between devices  163 us (47%)
  blocking collectives  47.2 us (14%)
  matrix products  45 us (13%)
  local copies, waits for them, and re-layouts  28.8 us (8%)
  starting transfers between devices  26 us (7%)
  between operations  18.9 us (5%)
  other arithmetic  18.8 us (5%)
    all_to_all x1, waiting for transfers between devices, gather_in_order(): lax.all_to_all(jnp.stack([blocks] * lax.axis_size(axes[k])), axes[k], 0, 0)  148 us
    all_to_all x2, blocking collectives, sent_to_all(): return lax.all_to_all(copies, axis, split_axis=0, concat_axis=0, tiled=True)  27.8 us
    all_to_all x2, starting transfers between devices, sent_to_all(): return lax.all_to_all(copies, axis, split_axis=0, concat_axis=0, tiled=True)  21.2 us
    all_to_all x1, blocking collectives, gather_in_order(): lax.all_to_all(jnp.stack([blocks] * lax.axis_size(axes[k])), axes[k], 0, 0)  19.5 us
    dot_general x1, matrix products, per_device(): product = jnp.dot(tokens, gathered, preferred_element_type=jnp.float32)  14.7 us
    dot_general x1, matrix products, per_device(): lax.dot_general(tokens, cotangent, (((0,), (0,)), ((), ())), preferred_el...  14.6 us
    dot_general x1, matrix products, per_device(): lax.dot_general(cotangent, gathered, (((1,), (1,)), ((), ())), preferred_...  13.8 us
    unnamed x12, local copies, waits for them, and re-layouts  12.8 us
  transfers between devices with their start and end apart: 4, of which 3 were waited for; matrix products, arithmetic and copies ran while one was open for 18% of the time, Pallas kernels for 0%

profile of v1, /device:TPU:1, one launch (start us, length us, event | category | flops | bytes accessed | tf_op | source)
XLA Modules:
  0.0 348.0 jit_solution(14830432353792261536)
XLA Ops:
  7.2 0.0 copy-start
  7.2 0.0 reduce-scatter.2.cloned.1.call-start
  7.2 1.5 copy-done
  8.8 14.6 %convolution_convert_fusion = bf16[4096,2048]{1,0:T(8,128)(2,1)} fusion(bf16[512,4096]{1,0:T(8,128)(2,1)} %param.4, bf16[512,2048]{1,0:T(8,128)(2,1)S(1)} %copy-done), kind=kOutput, calls=%fused_computation.1 | convolution fusion | flops 8598323200 | bytes 23068672 | tf_op jit(solution)/shard_map/dot_general | solution.py:75
  23.4 0.0 copy-start.1
  23.4 0.0 copy-start.4
  23.4 0.0 reduce-scatter.2.cloned.1.call-update
  23.4 1.0 copy-done.1
  24.4 0.0 copy-done.4
  24.4 0.2 fusion.8
  24.6 0.1 broadcast_in_dim.14
  24.8 17.3 %all_to_all.33 = f32[32,1,2048]{2,1,0:T(1,128)S(1)} all-to-all(f32[32,1,2048]{2,1,0:T(1,128)S(1)} %broadcast_in_dim.14), channel_id=1, replica_groups=mesh['fsdp_0'=4,'fsdp_1'=4,'fsdp_2'=2,'dp'=4] {'fsdp_0','fsdp_1','fsdp_2'}, dimensions={0} | all-to-all | bytes 524288 | tf_op jit(solution)/shard_map/all_to_all | solution.py:14
  42.1 0.2 reduce_sum.90
  42.3 0.6 multiply_reduce_fusion.3
  43.6 0.7 multiply_reduce_fusion.2
  44.2 0.0 copy-start.2
  44.2 0.8 multiply_reduce_fusion.4
  45.1 0.7 broadcast_in_dim.15
  45.8 10.4 %all_to_all.34 = f32[32,1,1]{2,1,0:T(1,128)S(1)} all-to-all(f32[32,1,1]{2,1,0:T(1,128)S(1)} %broadcast_in_dim.15), channel_id=1, replica_groups=mesh['fsdp_0'=4,'fsdp_1'=4,'fsdp_2'=2,'dp'=4] {'fsdp_0','fsdp_1','fsdp_2'}, dimensions={0} | all-to-all | bytes 256 | tf_op jit(solution)/shard_map/all_to_all | solution.py:14
  56.2 4.8 %stack.6 = bf16[16,1,128,2048]{3,2,1,0:T(8,128)(2,1)} broadcast(bf16[128,2048]{1,0:T(8,128)(2,1)S(1)} %copy-done.1), dimensions={2,3} | broadcast | bytes 8912896 | tf_op jit(solution)/shard_map/stack | solution.py:31
  61.0 4.8 %all-to-all-start = ((bf16[16,1,128,2048]{3,2,1,0:T(8,128)(2,1)}), bf16[16,1,128,2048]{3,2,1,0:T(8,128)(2,1)}, u32[]{:S(2)}, u32[]{:S(2)}) async-start(bf16[16,1,128,2048]{3,2,1,0:T(8,128)(2,1)} %stack.6), calls=%async_computation | async-start | bytes 16777216 | tf_op jit(solution)/shard_map/all_to_all | solution.py:31
  65.8 0.6 reduce_sum.93
  67.8 0.0 copy-start.3
  67.8 147.6 %all-to-all-done = bf16[16,1,128,2048]{3,2,1,0:T(8,128)(2,1)} async-done(((bf16[16,1,128,2048]{3,2,1,0:T(8,128)(2,1)}), bf16[16,1,128,2048]{3,2,1,0:T(8,128)(2,1)}, u32[]{:S(2)}, u32[]{:S(2)}) %all-to-all-start) | async-done | bytes 8388640 | tf_op jit(solution)/shard_map/all_to_all | solution.py:31
  215.4 9.7 %pad_maximum_fusion = bf16[2,16,128,2048]{3,2,1,0:T(8,128)(2,1)S(1)} fusion(bf16[1,16,128,2048]{3,2,1,0:T(8,128)(2,1)} %bitcast), kind=kLoop, calls=%fused_computation | loop fusion | flops 8388608 | bytes 25165824 | tf_op jit(solution)/shard_map/stack | solution.py:31
  225.1 19.5 %all_to_all.35 = bf16[2,16,128,2048]{3,2,1,0:T(8,128)(2,1)S(1)} all-to-all(bf16[2,16,128,2048]{3,2,1,0:T(8,128)(2,1)S(1)} %pad_maximum_fusion), channel_id=1, replica_groups=mesh['fsdp_0'=4,'fsdp_1'=4,'fsdp_2'=2,'dp'=4] {'fsdp_2'}, dimensions={0} | all-to-all | bytes 33554432 | tf_op jit(solution)/shard_map/all_to_all | solution.py:31
  244.6 6.6 %copy.25 = bf16[2,16,128,2048]{3,2,0,1:T(8,128)(2,1)} copy(bf16[2,16,128,2048]{3,2,1,0:T(8,128)(2,1)S(1)} %all_to_all.35) | data formatting | bytes 33554432 | tf_op jit(solution)/shard_map/all_to_all | solution.py:31
  251.2 5.9 %reduce-scatter.2.cloned.1.call-done = bf16[128,2048]{1,0:T(8,128)(2,1)} async-done(((bf16[4096,2048]{1,0:T(8,128)(2,1)}), bf16[128,2048]{1,0:T(8,128)(2,1)}) %reduce-scatter.2.cloned.1.call-update) | async-done | bytes 524304 | tf_op jit(solution)/shard_map/reduce_scatter | solution.py:74
  257.1 2.6 broadcast_in_dim.16
  259.7 4.6 %all-to-all-start.4 = ((bf16[4,128,2048]{2,1,0:T(8,128)(2,1)}), bf16[4,128,2048]{2,1,0:T(8,128)(2,1)}, u32[]{:S(2)}, u32[]{:S(2)}) async-start(bf16[4,128,2048]{2,1,0:T(8,128)(2,1)} %broadcast_in_dim.16), calls=%async_computation.5 | async-start | bytes 4194304 | tf_op jit(solution)/shard_map/all_to_all | solution.py:14
  264.3 14.7 %fusion.1 = bf16[512,2048]{0,1:T(8,128)(2,1)} fusion(bf16[4096,2048]{1,0:T(8,128)(2,1)} %bitcast.48, bf16[512,4096]{1,0:T(8,128)(2,1)} %param.4, f32[]{:T(128)S(6)} %sqrt.10), kind=kOutput, calls=%fused_computation.6 | convolution fusion | flops 8592031744 | bytes 23068676 | tf_op jit(solution)/shard_map/dot_general | solution.py:67
  279.0 9.7 %all-to-all-done.4 = bf16[4,128,2048]{2,1,0:T(8,128)(2,1)} async-done(((bf16[4,128,2048]{2,1,0:T(8,128)(2,1)}), bf16[4,128,2048]{2,1,0:T(8,128)(2,1)}, u32[]{:S(2)}, u32[]{:S(2)}) %all-to-all-start.4) | async-done | bytes 2097184 | tf_op jit(solution)/shard_map/all_to_all | solution.py:14
  288.7 2.1 convert_reduce_fusion
  290.8 1.9 multiply_reduce_fusion.1
  292.7 0.0 copy-done.3
  292.7 0.8 fusion.3
  293.5 1.9 pad_maximum_fusion.1
  295.4 0.6 broadcast_in_dim.17
  296.1 16.6 %all-to-all-start.5 = ((f32[32,1,3]{2,1,0:T(1,128)}), f32[32,1,3]{2,1,0:T(1,128)S(1)}, u32[]{:S(2)}, u32[]{:S(2)}) async-start(f32[32,1,3]{2,1,0:T(1,128)} %broadcast_in_dim.17), calls=%async_computation.6 | async-start | bytes 32768 | tf_op jit(solution)/shard_map/all_to_all | solution.py:14
  312.7 13.8 %fusion = bf16[512,4096]{0,1:T(8,128)(2,1)} fusion(bf16[4096,2048]{1,0:T(8,128)(2,1)} %bitcast.49, bf16[512,2048]{1,0:T(8,128)(2,1)S(1)} %copy-done, f32[]{:T(128)S(6)} %sqrt.10), kind=kOutput, calls=%fused_computation.3 | convolution fusion | flops 8594128896 | bytes 23068676 | tf_op jit(solution)/shard_map/dot_general | solution.py:69
  326.5 3.9 %copy.29 = bf16[512,2048]{1,0:T(8,128)(2,1)} copy(bf16[512,2048]{0,1:T(8,128)(2,1)} %fusion.1) | data formatting | bytes 4194304
  330.4 6.3 %copy.30 = bf16[512,4096]{1,0:T(8,128)(2,1)} copy(bf16[512,4096]{0,1:T(8,128)(2,1)} %fusion) | data formatting | bytes 8388608
  336.7 0.0 all-to-all-done.5
  336.7 0.1 reduce_sum.98
  336.8 0.6 fusion.7
  340.1 0.0 copy-done.2
  340.1 1.0 divide_convert_fusion.2
  (2 shorter events, 0.0 us)
Async XLA Ops:
  7.2 1.6 copy-start
  7.2 249.9 %reduce-scatter.2.cloned.1.call-start = ((), (), s32[]{:S(2)}) async-start(), calls=%async_computation.7 | async-start | bytes 17301504 | tf_op jit(solution)/shard_map/reduce_scatter | solution.py:74
  23.4 1.0 copy-start.1
  23.4 1.0 copy-start.4
  44.2 295.9 %copy-start.2 = (f32[2048]{0:T(1024)}, f32[2048]{0:T(1024)S(1)}, u32[]{:S(2)}) copy-start(f32[2048]{0:T(1024)S(1)} %get-tuple-element.38) | copy-start | bytes 24580
  61.0 154.4 %all-to-all-start = ((bf16[16,1,128,2048]{3,2,1,0:T(8,128)(2,1)}), bf16[16,1,128,2048]{3,2,1,0:T(8,128)(2,1)}, u32[]{:S(2)}, u32[]{:S(2)}) async-start(bf16[16,1,128,2048]{3,2,1,0:T(8,128)(2,1)} %stack.6), calls=%async_computation | async-start | bytes 16777216 | tf_op jit(solution)/shard_map/all_to_all | solution.py:31
  67.8 224.9 %copy-start.3 = (f32[128]{0:T(128)}, f32[128]{0:T(128)S(1)}, u32[]{:S(2)}) copy-start(f32[128]{0:T(128)S(1)} %broadcast_divide_fusion.1) | copy-start | bytes 1540
  259.7 29.0 %all-to-all-start.4 = ((bf16[4,128,2048]{2,1,0:T(8,128)(2,1)}), bf16[4,128,2048]{2,1,0:T(8,128)(2,1)}, u32[]{:S(2)}, u32[]{:S(2)}) async-start(bf16[4,128,2048]{2,1,0:T(8,128)(2,1)} %broadcast_in_dim.16), calls=%async_computation.5 | async-start | bytes 4194304 | tf_op jit(solution)/shard_map/all_to_all | solution.py:14
  296.1 40.7 %all-to-all-start.5 = ((f32[32,1,3]{2,1,0:T(1,128)}), f32[32,1,3]{2,1,0:T(1,128)S(1)}, u32[]{:S(2)}, u32[]{:S(2)}) async-start(f32[32,1,3]{2,1,0:T(1,128)} %broadcast_in_dim.17), calls=%async_computation.6 | async-start | bytes 32768 | tf_op jit(solution)/shard_map/all_to_all | solution.py:14
Sparse Core Ops, SparseCore 0:
  23.5 233.4 reduce-scatter.1
